TPU v7x, 32 devices: a whole 2x2x4 slice. The times are simulated.
32 devices in a mesh: fsdp: 16 (over z, y, x), tp: 2 (over core).
Axes of the slice: x: 2, y: 2, z: 4, core: 2. Of those that a mesh axis runs over, the one named last changes fastest.
Arguments:
- inputs: bfloat16 [4096, 4096], P('fsdp'), may hold values from -6 to 6
- value_grad: bfloat16 [4096, 1024], P('fsdp', 'tp'), may hold values from -24 to 24
- value_weight: bfloat16 [4096, 1024], P('tp', 'fsdp'), may hold values from -0.09375 to 0.09375
- counts: int32 [16, 4], P('fsdp'), may hold values from 1 to 232, as said below
- offsets: int32 [16, 4], P('fsdp'), may hold values from 0 to 248, as said below
Outputs:
- input_grad: bfloat16 [4096, 4096], P('fsdp', 'tp')
- weight_grad: float32 [4096, 1024], P('fsdp', 'tp')
Inputs may be any that keep to these rules, and one draw needn't show every extreme that they name: `offsets`: on each index of fsdp the 4 samples lie in order; each starts at a multiple of 8, at or after the 8-row-aligned end of the previous one, and all lie within the 256 rows; on some index the aligned blocks of its samples fill all 256 rows. `counts`: how many rows the samples of a row group fill varies widely between indices of fsdp.
All inputs are finite; a program needn't handle non-finite values.
Results may differ from a plain program's by a relative error of at most 0.0046.
Values may be sent and summed in bfloat16 or wider, within the bound.
A program may use at most 64 MiB of HBM per device.

v0:
```python
import math
import jax
import jax.numpy as jnp
from jax import lax
from jax.sharding import PartitionSpec as P


def local(inputs, value_grad, value_weight, counts, offsets):
    tok_rows = inputs.shape[0]
    row_block = min(128, tok_rows)
    positions = jnp.arange(tok_rows, dtype=jnp.int32)[:, None]
    starts = offsets[0][None, :]
    lengths = counts[0][None, :]
    inside = (positions >= starts) & (positions < starts + lengths)
    inverse_root = lax.rsqrt(lengths.astype(jnp.float32))
    row_factor = jnp.sum(jnp.where(inside, inverse_root, jnp.zeros_like(inverse_root)), axis=1)
    scaled = (value_grad.astype(jnp.float32) * row_factor[:, None]).astype(jnp.bfloat16)
    live_end = jnp.max(offsets[0] + counts[0])
    live_blocks = (live_end + row_block - 1) // row_block
    scaled_all = lax.all_gather(scaled, "tp", axis=1, tiled=True)
    empty_inputs = jnp.zeros((tok_rows, value_weight.shape[0]), jnp.float32)
    piece = lax.all_gather(value_weight, "fsdp", axis=1, tiled=True)

    def add_add_block(block_index, partial_value):
        lower = lax.dynamic_slice_in_dim(scaled_all, block_index * row_block, row_block, 0)
        before = lax.dynamic_slice_in_dim(partial_value, block_index * row_block, row_block, 0)
        product = lax.dot_general(
            lower, piece, (((1,), (1,)), ((), ())), preferred_element_type=jnp.float32
        )
        return lax.dynamic_update_slice_in_dim(
            partial_value, before + product, block_index * row_block, 0
        )

    result = lax.fori_loop(0, live_blocks, add_add_block, empty_inputs)
    input_grad = result.astype(jnp.bfloat16)
    normalizer = 1.0 / math.sqrt(counts.shape[1] * lax.axis_size("fsdp"))
    empty = jnp.zeros((inputs.shape[1], scaled.shape[1]), jnp.float32)

    def weight_add_block(block_index, partial_value):
        feature_rows = lax.dynamic_slice_in_dim(inputs, block_index * row_block, row_block, 0)
        grad_rows = lax.dynamic_slice_in_dim(scaled, block_index * row_block, row_block, 0)
        return partial_value + lax.dot_general(
            feature_rows, grad_rows, (((0,), (0,)), ((), ())), preferred_element_type=jnp.float32
        )

    result = lax.fori_loop(0, live_blocks, weight_add_block, empty)
    summed = lax.psum_scatter(result, "fsdp", scatter_dimension=0, tiled=True)
    return (input_grad, summed * normalizer)


def solution(mesh):
    in_specs = (P("fsdp", None), P("fsdp", "tp"), P("tp", "fsdp"), P("fsdp", None), P("fsdp", None))
    out_specs = (P("fsdp", "tp"), P("fsdp", "tp"))
    return jax.shard_map(local, mesh=mesh, in_specs=in_specs, out_specs=out_specs, check_vma=False)
```

profile of v0, /device:TPU:10, one launch (start us, length us, event | category | flops | bytes accessed | tf_op | source)
XLA Modules:
  0.0 278.1 jit_solution(10683928178615963049)
XLA Ops:
  7.2 0.0 all-gather.2.cloned.1.call-start
  7.2 0.7 all-gather.2.cloned.1.call-update
  7.9 0.0 reduce-scatter.2.cloned.1.call-start
  7.9 1.3 fusion.7
  9.9 0.7 rsqrt_bitcast_fusion
  10.6 0.7 add_bitcast_fusion
  11.3 0.7 select_reduce_fusion
  12.0 1.1 multiply_convert_fusion
  13.1 0.0 copy-start
  13.1 4.3 %broadcast_in_dim.30 = f32[4096,512]{1,0:T(8,128)} broadcast(f32[]{:T(128)} %constant.38.clone.1), dimensions={} | broadcast | bytes 8388612 | tf_op jit(solution)/shard_map/broadcast_in_dim | solution.py:37
  17.4 0.0 copy-done
  17.4 8.0 %while.21 = (s32[]{:T(128)}, f32[4096,512]{1,0:T(8,128)}, s32[]{:T(128)}, bf16[256,4096]{1,0:T(8,128)(2,1)S(1)}, bf16[256,512]{1,0:T(8,128)(2,1)S(1)}, /*index=5*/s32[]{:T(128)}, s32[]{:T(128)}, s32[]{:T(128)}, s32[]{:T(128)}) while((s32[]{:T(128)}, f32[4096,512]{1,0:T(8,128)}, s32[]{:T(128)}, bf16[256,4096]{1,0:T(8,128)(2,1)S(1)}, ...), condition=%wide.region_5.6_spmd, body=%wide.region_4.5_spmd.sunk | while | flops 538968064 | bytes 17958028 | solution.py:46
  17.4 8.0 %convolution_add_fusion.3 = f32[4096,512]{1,0:T(8,128)} fusion(f32[4096,512]{1,0:T(8,128)} %get-tuple-element.191, bf16[256,4096]{1,0:T(8,128)(2,1)S(1)} %get-tuple-element.202, s32[]{:T(128)S(6)} %select_n.24, bf16[256,512]{1,0:T(8,128)(2,1)S(1)} %get-tuple-element.203), kind=kOutput, calls=%fused_computation.4.clone.1 | convolution fusion | flops 538968064 | bytes 17957888 | tf_op jit(solution)/shard_map/while/body/dot_general | solution.py:42
  25.4 0.0 reduce-scatter.2.cloned.1.call-update
  25.4 2.2 all_gather.6
  27.6 59.9 %all-gather.2.cloned.1.call-done = bf16[2048,1024]{0,1:T(8,128)(2,1)} async-done(((bf16[2048,64]{0,1:T(8,128)(2,1)}), bf16[2048,1024]{0,1:T(8,128)(2,1)}) %all-gather.2.cloned.1.call-update) | async-done | bytes 4194320 | tf_op jit(solution)/shard_map/all_gather | solution.py:22
  87.5 6.4 %copy.9 = bf16[2048,1024]{1,0:T(8,128)(2,1)} copy(bf16[2048,1024]{0,1:T(8,128)(2,1)} %all-gather.2.cloned.1.call-done) | data formatting | bytes 8388608 | tf_op jit(solution)/shard_map/while | solution.py:34
  93.9 0.2 broadcast_in_dim.26
  94.1 4.0 %while.20 = (s32[]{:T(128)}, f32[256,2048]{1,0:T(8,128)S(1)}, s32[]{:T(128)}, bf16[256,1024]{1,0:T(8,128)(2,1)S(1)}, bf16[2048,1024]{1,0:T(8,128)(2,1)}, /*index=5*/s32[]{:T(128)}, s32[]{:T(128)}, s32[]{:T(128)}, s32[]{:T(128)}) while((s32[]{:T(128)}, f32[256,2048]{1,0:T(8,128)S(1)}, s32[]{:T(128)}, bf16[256,1024]{1,0:T(8,128)(2,1)S(1)}, ...), condition=%wide.region_3.4_spmd, body=%wide.region_2.3_spmd.sunk | while | flops 537133056 | bytes 6554763 | solution.py:34
  94.2 4.0 %fusion.16 = f32[256,2048]{1,0:T(8,128)S(1)} fusion(f32[256,2048]{1,0:T(8,128)S(1)} %get-tuple-element.164, s32[]{:T(128)S(6)} %select_n.23, bf16[2048,1024]{1,0:T(8,128)(2,1)} %get-tuple-element.176, bf16[256,1024]{1,0:T(8,128)(2,1)S(1)} %get-tuple-element.175), kind=kOutput, calls=%fused_computation.1.clone.1 | convolution fusion | flops 537133056 | bytes 6554624 | tf_op jit(solution)/shard_map/while/body/dot_general | solution.py:27
  98.1 1.1 convert_element_type.15
  99.3 170.2 %reduce-scatter.2.cloned.1.call-done = f32[256,512]{1,0:T(8,128)} async-done(((f32[4096,512]{1,0:T(8,128)}), f32[256,512]{1,0:T(8,128)}) %reduce-scatter.2.cloned.1.call-update) | async-done | bytes 524304 | tf_op jit(solution)/shard_map/reduce_scatter | solution.py:47
  269.4 1.9 broadcast_multiply_fusion
Async XLA Ops:
  7.2 80.3 %all-gather.2.cloned.1.call-start = ((), (), s32[]{:S(2)}) async-start(), calls=%async_computation.1 | async-start | bytes 4456448 | tf_op jit(solution)/shard_map/all_gather | solution.py:22
  7.9 261.5 %reduce-scatter.2.cloned.1.call-start = ((), (), s32[]{:S(2)}) async-start(), calls=%async_computation.2 | async-start | bytes 8912896 | tf_op jit(solution)/shard_map/reduce_scatter | solution.py:47
  13.1 4.3 %copy-start = (bf16[256,4096]{1,0:T(8,128)(2,1)S(1)}, bf16[256,4096]{1,0:T(8,128)(2,1)}, u32[]{:S(2)}) copy-start(bf16[256,4096]{1,0:T(8,128)(2,1)} %param.9) | copy-start | bytes 6291460
Sparse Core Ops, SparseCore 0:
  10.7 76.6 all-gather.1
  89.8 179.6 reduce-scatter.1
where the time goes:
time: 279 us; the launch traced here: 278 us
  waiting for transfers between devices  231 us (83%)
  between operations  14.7 us (5%)
  matrix products  12 us (4%)
  local copies, waits for them, and re-layouts  10.9 us (4%)
  other arithmetic  7.43 us (3%)
    reduce_scatter x1, waiting for transfers between devices, local(): summed = lax.psum_scatter(result, 'fsdp', scatter_dimension=0, tiled=True)  170 us
    all_gather x1, waiting for transfers between devices, local(): piece = lax.all_gather(value_weight, 'fsdp', axis=1, tiled=True)  59.9 us
    dot_general x1, matrix products, weight_add_block(): lax.dot_general(feature_rows, grad_rows, (((0,), (0,)), ((), ())), prefer...  7.98 us
    while x1, local copies, waits for them, and re-layouts, local(): result = lax.fori_loop(0, live_blocks, add_add_block, empty_inputs)  6.42 us
  transfers between devices with their start and end apart: 2, of which 2 were waited for; matrix products, arithmetic and copies ran while one was open for 10% of the time, Pallas kernels for 0%

commit v1 on v0

--- a/solution.py
+++ b/solution.py
@@ -3,6 +3,16 @@
 import jax.numpy as jnp
 from jax import lax
 from jax.sharding import PartitionSpec as P
+
+
+def around_the_ring(x, name, dim):
+    size = lax.axis_size(name)
+    moving, blocks = (x, [x])
+    for _ in range(size - 1):
+        moving = lax.ppermute(moving, name, [(i, (i + 1) % size) for i in range(size)])
+        blocks.insert(0, moving)
+    line = jnp.concatenate(blocks, axis=dim)
+    return jnp.roll(line, (lax.axis_index(name) + 1) * x.shape[dim], axis=dim)
 
 
 def local(inputs, value_grad, value_weight, counts, offsets):
@@ -19,7 +29,7 @@
     live_blocks = (live_end + row_block - 1) // row_block
     scaled_all = lax.all_gather(scaled, "tp", axis=1, tiled=True)
     empty_inputs = jnp.zeros((tok_rows, value_weight.shape[0]), jnp.float32)
-    piece = lax.all_gather(value_weight, "fsdp", axis=1, tiled=True)
+    piece = around_the_ring(value_weight, "fsdp", 1)
 
     def add_add_block(block_index, partial_value):
         lower = lax.dynamic_slice_in_dim(scaled_all, block_index * row_block, row_block, 0)

time: 279 us -> 449 us (1.61)
  the two profiles are of different devices: /device:TPU:10 before, /device:TPU:16 now
where the time goes in v1:
time: 449 us; the launch traced here: 447 us
  waiting for transfers between devices  325 us (72%)
  local copies, waits for them, and re-layouts  39.6 us (9%)
  starting transfers between devices  33.9 us (8%)
  matrix products  23.2 us (5%)
  between operations  14.8 us (3%)
  other arithmetic  7.43 us (2%)
    ppermute x15, waiting for transfers between devices, around_the_ring(): lax.ppermute(moving, name, [(i, (i + 1) % size) for i in range(size)])  325 us
    ppermute x15, starting transfers between devices, around_the_ring(): lax.ppermute(moving, name, [(i, (i + 1) % size) for i in range(size)])  33.9 us
    concatenate x1, local copies, waits for them, and re-layouts, around_the_ring(): return jnp.roll(line, (lax.axis_index(name) + 1) * x.shape[dim], axis=dim)  20.2 us
    dot_general x2, matrix products, weight_add_block(): lax.dot_general(feature_rows, grad_rows, (((0,), (0,)), ((), ())), prefer...  15.8 us
  transfers between devices with their start and end apart: 16, of which 15 were waited for; matrix products, arithmetic and copies ran while one was open for 8% of the time, Pallas kernels for 0%

profile of v1, /device:TPU:16, one launch (start us, length us, event | category | flops | bytes accessed | tf_op | source)
XLA Modules:
  0.0 446.5 jit_solution(11944555968389722837)
XLA Ops:
  12.3 4.3 broadcast_in_dim.30
  16.6 15.8 %while.21 = (s32[]{:T(128)}, f32[4096,512]{1,0:T(8,128)}, s32[]{:T(128)}, bf16[256,4096]{1,0:T(8,128)(2,1)S(1)}, bf16[256,512]{1,0:T(8,128)(2,1)S(1)}, /*index=5*/s32[]{:T(128)}, s32[]{:T(128)}, s32[]{:T(128)}, s32[]{:T(128)}) while((s32[]{:T(128)}, f32[4096,512]{1,0:T(8,128)}, s32[]{:T(128)}, bf16[256,4096]{1,0:T(8,128)(2,1)S(1)}, ...), condition=%wide.region_5.6_spmd, body=%wide.region_4.5_spmd.sunk | while | flops 538968064 | bytes 17958028 | solution.py:56
  16.6 7.9 %convolution_add_fusion.3 = f32[4096,512]{1,0:T(8,128)} fusion(f32[4096,512]{1,0:T(8,128)} %get-tuple-element.181, bf16[256,4096]{1,0:T(8,128)(2,1)S(1)} %get-tuple-element.192, s32[]{:T(128)S(6)} %select_n.38, bf16[256,512]{1,0:T(8,128)(2,1)S(1)} %get-tuple-element.193), kind=kOutput, calls=%fused_computation.4.clone.1 | convolution fusion | flops 538968064 | bytes 17957888 | tf_op jit(solution)/shard_map/while/body/dot_general | solution.py:52
  24.5 7.9 %convolution_add_fusion.3 = f32[4096,512]{1,0:T(8,128)} fusion(f32[4096,512]{1,0:T(8,128)} %get-tuple-element.181, bf16[256,4096]{1,0:T(8,128)(2,1)S(1)} %get-tuple-element.192, s32[]{:T(128)S(6)} %select_n.38, bf16[256,512]{1,0:T(8,128)(2,1)S(1)} %get-tuple-element.193), kind=kOutput, calls=%fused_computation.4.clone.1 | convolution fusion | flops 538968064 | bytes 17957888 | tf_op jit(solution)/shard_map/while/body/dot_general | solution.py:52
  33.7 30.3 %collective-permute-done = bf16[2048,64]{1,0:T(8,128)(2,1)S(1)} collective-permute-done((bf16[2048,64]{1,0:T(8,128)(2,1)S(1)}, bf16[2048,64]{1,0:T(8,128)(2,1)S(1)}, u32[]{:S(2)}, u32[]{:S(2)}) %collective-permute-start) | collective-permute-done | bytes 262176 | tf_op jit(solution)/shard_map/ppermute | solution.py:12
  64.0 2.5 collective-permute-start.1
  66.5 32.9 %collective-permute-done.1 = bf16[2048,64]{1,0:T(8,128)(2,1)S(1)} collective-permute-done((bf16[2048,64]{1,0:T(8,128)(2,1)S(1)}, bf16[2048,64]{1,0:T(8,128)(2,1)S(1)}, u32[]{:S(2)}, u32[]{:S(2)}) %collective-permute-start.1) | collective-permute-done | bytes 262176 | tf_op jit(solution)/shard_map/ppermute | solution.py:12
  101.9 32.7 %collective-permute-done.2 = bf16[2048,64]{1,0:T(8,128)(2,1)S(1)} collective-permute-done((bf16[2048,64]{1,0:T(8,128)(2,1)S(1)}, bf16[2048,64]{1,0:T(8,128)(2,1)S(1)}, u32[]{:S(2)}, u32[]{:S(2)}) %collective-permute-start.2) | collective-permute-done | bytes 262176 | tf_op jit(solution)/shard_map/ppermute | solution.py:12
  137.0 34.1 %collective-permute-done.3 = bf16[2048,64]{1,0:T(8,128)(2,1)S(1)} collective-permute-done((bf16[2048,64]{1,0:T(8,128)(2,1)S(1)}, bf16[2048,64]{1,0:T(8,128)(2,1)S(1)}, u32[]{:S(2)}, u32[]{:S(2)}) %collective-permute-start.3) | collective-permute-done | bytes 262176 | tf_op jit(solution)/shard_map/ppermute | solution.py:12
  171.1 4.4 collective-permute-start.4
  175.5 31.1 %collective-permute-done.4 = bf16[2048,64]{1,0:T(8,128)(2,1)S(1)} collective-permute-done((bf16[2048,64]{1,0:T(8,128)(2,1)S(1)}, bf16[2048,64]{1,0:T(8,128)(2,1)S(1)}, u32[]{:S(2)}, u32[]{:S(2)}) %collective-permute-start.4) | collective-permute-done | bytes 262176 | tf_op jit(solution)/shard_map/ppermute | solution.py:12
  207.4 4.2 collective-permute-start.5
  211.6 31.4 %collective-permute-done.5 = bf16[2048,64]{1,0:T(8,128)(2,1)S(1)} collective-permute-done((bf16[2048,64]{1,0:T(8,128)(2,1)S(1)}, bf16[2048,64]{1,0:T(8,128)(2,1)S(1)}, u32[]{:S(2)}, u32[]{:S(2)}) %collective-permute-start.5) | collective-permute-done | bytes 262176 | tf_op jit(solution)/shard_map/ppermute | solution.py:12
  243.8 2.5 collective-permute-start.6
  246.2 33.6 %collective-permute-done.6 = bf16[2048,64]{1,0:T(8,128)(2,1)S(1)} collective-permute-done((bf16[2048,64]{1,0:T(8,128)(2,1)S(1)}, bf16[2048,64]{1,0:T(8,128)(2,1)S(1)}, u32[]{:S(2)}, u32[]{:S(2)}) %collective-permute-start.6) | collective-permute-done | bytes 262176 | tf_op jit(solution)/shard_map/ppermute | solution.py:12
  280.6 2.5 collective-permute-start.7
  283.1 13.6 %collective-permute-done.7 = bf16[2048,64]{1,0:T(8,128)(2,1)S(1)} collective-permute-done((bf16[2048,64]{1,0:T(8,128)(2,1)S(1)}, bf16[2048,64]{1,0:T(8,128)(2,1)S(1)}, u32[]{:S(2)}, u32[]{:S(2)}) %collective-permute-start.7) | collective-permute-done | bytes 262176 | tf_op jit(solution)/shard_map/ppermute | solution.py:12
  297.5 2.9 collective-permute-start.8
  300.4 10.8 %collective-permute-done.8 = bf16[2048,64]{1,0:T(8,128)(2,1)S(1)} collective-permute-done((bf16[2048,64]{1,0:T(8,128)(2,1)S(1)}, bf16[2048,64]{1,0:T(8,128)(2,1)S(1)}, u32[]{:S(2)}, u32[]{:S(2)}) %collective-permute-start.8) | collective-permute-done | bytes 262176 | tf_op jit(solution)/shard_map/ppermute | solution.py:12
  312.0 3.5 collective-permute-start.9
  315.5 11.7 %collective-permute-done.9 = bf16[2048,64]{1,0:T(8,128)(2,1)S(1)} collective-permute-done((bf16[2048,64]{1,0:T(8,128)(2,1)S(1)}, bf16[2048,64]{1,0:T(8,128)(2,1)S(1)}, u32[]{:S(2)}, u32[]{:S(2)}) %collective-permute-start.9) | collective-permute-done | bytes 262176 | tf_op jit(solution)/shard_map/ppermute | solution.py:12
  328.0 3.7 collective-permute-start.10
  331.7 12.6 %collective-permute-done.10 = bf16[2048,64]{1,0:T(8,128)(2,1)S(1)} collective-permute-done((bf16[2048,64]{1,0:T(8,128)(2,1)S(1)}, bf16[2048,64]{1,0:T(8,128)(2,1)S(1)}, u32[]{:S(2)}, u32[]{:S(2)}) %collective-permute-start.10) | collective-permute-done | bytes 262176 | tf_op jit(solution)/shard_map/ppermute | solution.py:12
  347.3 13.5 %collective-permute-done.11 = bf16[2048,64]{1,0:T(8,128)(2,1)S(1)} collective-permute-done((bf16[2048,64]{1,0:T(8,128)(2,1)S(1)}, bf16[2048,64]{1,0:T(8,128)(2,1)S(1)}, u32[]{:S(2)}, u32[]{:S(2)}) %collective-permute-start.11) | collective-permute-done | bytes 262176 | tf_op jit(solution)/shard_map/ppermute | solution.py:12
  362.1 14.5 %collective-permute-done.12 = bf16[2048,64]{1,0:T(8,128)(2,1)S(1)} collective-permute-done((bf16[2048,64]{1,0:T(8,128)(2,1)S(1)}, bf16[2048,64]{1,0:T(8,128)(2,1)S(1)}, u32[]{:S(2)}, u32[]{:S(2)}) %collective-permute-start.12) | collective-permute-done | bytes 262176 | tf_op jit(solution)/shard_map/ppermute | solution.py:12
  377.4 13.6 %collective-permute-done.13 = bf16[2048,64]{1,0:T(8,128)(2,1)} collective-permute-done((bf16[2048,64]{1,0:T(8,128)(2,1)S(1)}, bf16[2048,64]{1,0:T(8,128)(2,1)}, u32[]{:S(2)}, u32[]{:S(2)}) %collective-permute-start.13) | collective-permute-done | bytes 262176 | tf_op jit(solution)/shard_map/ppermute | solution.py:12
  393.1 9.1 %collective-permute-done.14 = bf16[2048,64]{1,0:T(8,128)(2,1)} collective-permute-done((bf16[2048,64]{1,0:T(8,128)(2,1)}, bf16[2048,64]{1,0:T(8,128)(2,1)}, u32[]{:S(2)}, u32[]{:S(2)}) %collective-permute-start.14) | collective-permute-done | bytes 262176 | tf_op jit(solution)/shard_map/ppermute | solution.py:12
  402.3 20.2 %concatenate.6 = bf16[2048,2048]{1,0:T(8,128)(2,1)} concatenate(bf16[2048,64]{1,0:T(8,128)(2,1)} %collective-permute-done.14, bf16[2048,64]{1,0:T(8,128)(2,1)} %collective-permute-done.13, bf16[2048,64]{1,0:T(8,128)(2,1)} %copy-done.9, bf16[2048,64]{1,0:T(8,128)(2,1)} %copy-done.8, bf16[2048,64]{1,0:T(8,128)(2,1)} %copy-done.7, bf16[2048,64]{1,0:T(8,128)(2,1)} %copy-done.6, ...), dimensions={1} | concatenate | bytes 16777216 | tf_op jit(solution)/shard_map/jit(_roll_dynamic)/concatenate | solution.py:15
  422.5 6.5 %constant_dynamic-slice_fusion = bf16[2048,1024]{1,0:T(8,128)(2,1)} fusion(bf16[2048,2048]{1,0:T(8,128)(2,1)} %concatenate.6, s32[]{:T(128)S(6)} %select_n.33), kind=kLoop, calls=%fused_computation.18 | loop fusion | bytes 8388612 | tf_op jit(solution)/shard_map/jit(_roll_dynamic)/dynamic_slice | solution.py:15
  429.2 7.5 %while.20 = (s32[]{:T(128)}, f32[256,2048]{1,0:T(8,128)S(1)}, s32[]{:T(128)}, bf16[256,1024]{1,0:T(8,128)(2,1)S(1)}, bf16[2048,1024]{1,0:T(8,128)(2,1)}, /*index=5*/s32[]{:T(128)}, s32[]{:T(128)}, s32[]{:T(128)}, s32[]{:T(128)}) while((s32[]{:T(128)}, f32[256,2048]{1,0:T(8,128)S(1)}, s32[]{:T(128)}, bf16[256,1024]{1,0:T(8,128)(2,1)S(1)}, ...), condition=%wide.region_3.4_spmd, body=%wide.region_2.3_spmd.sunk | while | flops 537133056 | bytes 6554763 | solution.py:44
  429.2 3.7 fusion.16
  432.9 3.7 fusion.16
  (42 shorter events, 26.0 us)
Async XLA Ops:
  7.2 430.6 %reduce-scatter.2.cloned.1.call-start = ((), (), s32[]{:S(2)}) async-start(), calls=%async_computation.1 | async-start | bytes 8912896 | tf_op jit(solution)/shard_map/reduce_scatter | solution.py:57
  12.3 4.3 copy-start
  32.4 0.9 copy-start.10
  33.6 30.4 %collective-permute-start = (bf16[2048,64]{1,0:T(8,128)(2,1)S(1)}, bf16[2048,64]{1,0:T(8,128)(2,1)S(1)}, u32[]{:S(2)}, u32[]{:S(2)}) collective-permute-start(bf16[2048,64]{1,0:T(8,128)(2,1)S(1)} %copy.10), channel_id=1, source_target_pairs={{0,2},{2,4},{4,6},{6,8},{8,10},{10,12},{12,14},{14,16},{16,18},{18... | collective-permute-start | bytes 786440 | tf_op jit(solution)/shard_map/ppermute | solution.py:12
  64.0 35.4 %collective-permute-start.1 = (bf16[2048,64]{1,0:T(8,128)(2,1)S(1)}, bf16[2048,64]{1,0:T(8,128)(2,1)S(1)}, u32[]{:S(2)}, u32[]{:S(2)}) collective-permute-start(bf16[2048,64]{1,0:T(8,128)(2,1)S(1)} %collective-permute-done), channel_id=1, source_target_pairs={{0,2},{2,4},{4,6},{6,8},{8,10},{10,12},{12,14},{14,16},{16,18},{18... | collective-permute-start | bytes 786440 | tf_op jit(solution)/shard_map/ppermute | solution.py:12
  99.4 35.2 %collective-permute-start.2 = (bf16[2048,64]{1,0:T(8,128)(2,1)S(1)}, bf16[2048,64]{1,0:T(8,128)(2,1)S(1)}, u32[]{:S(2)}, u32[]{:S(2)}) collective-permute-start(bf16[2048,64]{1,0:T(8,128)(2,1)S(1)} %collective-permute-done.1), channel_id=1, source_target_pairs={{0,2},{2,4},{4,6},{6,8},{8,10},{10,12},{12,14},{14,16},{16,18},{18... | collective-permute-start | bytes 786440 | tf_op jit(solution)/shard_map/ppermute | solution.py:12
  134.6 36.6 %collective-permute-start.3 = (bf16[2048,64]{1,0:T(8,128)(2,1)S(1)}, bf16[2048,64]{1,0:T(8,128)(2,1)S(1)}, u32[]{:S(2)}, u32[]{:S(2)}) collective-permute-start(bf16[2048,64]{1,0:T(8,128)(2,1)S(1)} %collective-permute-done.2), channel_id=1, source_target_pairs={{0,2},{2,4},{4,6},{6,8},{8,10},{10,12},{12,14},{14,16},{16,18},{18... | collective-permute-start | bytes 786440 | tf_op jit(solution)/shard_map/ppermute | solution.py:12
  171.1 35.5 %collective-permute-start.4 = (bf16[2048,64]{1,0:T(8,128)(2,1)S(1)}, bf16[2048,64]{1,0:T(8,128)(2,1)S(1)}, u32[]{:S(2)}, u32[]{:S(2)}) collective-permute-start(bf16[2048,64]{1,0:T(8,128)(2,1)S(1)} %collective-permute-done.3), channel_id=1, source_target_pairs={{0,2},{2,4},{4,6},{6,8},{8,10},{10,12},{12,14},{14,16},{16,18},{18... | collective-permute-start | bytes 786440 | tf_op jit(solution)/shard_map/ppermute | solution.py:12
  206.6 0.8 copy-start.1
  207.4 35.6 %collective-permute-start.5 = (bf16[2048,64]{1,0:T(8,128)(2,1)S(1)}, bf16[2048,64]{1,0:T(8,128)(2,1)S(1)}, u32[]{:S(2)}, u32[]{:S(2)}) collective-permute-start(bf16[2048,64]{1,0:T(8,128)(2,1)S(1)} %collective-permute-done.4), channel_id=1, source_target_pairs={{0,2},{2,4},{4,6},{6,8},{8,10},{10,12},{12,14},{14,16},{16,18},{18... | collective-permute-start | bytes 786440 | tf_op jit(solution)/shard_map/ppermute | solution.py:12
  243.0 0.8 copy-start.2
  243.8 36.1 %collective-permute-start.6 = (bf16[2048,64]{1,0:T(8,128)(2,1)S(1)}, bf16[2048,64]{1,0:T(8,128)(2,1)S(1)}, u32[]{:S(2)}, u32[]{:S(2)}) collective-permute-start(bf16[2048,64]{1,0:T(8,128)(2,1)S(1)} %collective-permute-done.5), channel_id=1, source_target_pairs={{0,2},{2,4},{4,6},{6,8},{8,10},{10,12},{12,14},{14,16},{16,18},{18... | collective-permute-start | bytes 786440 | tf_op jit(solution)/shard_map/ppermute | solution.py:12
  279.8 0.8 copy-start.3
  280.6 16.0 %collective-permute-start.7 = (bf16[2048,64]{1,0:T(8,128)(2,1)S(1)}, bf16[2048,64]{1,0:T(8,128)(2,1)S(1)}, u32[]{:S(2)}, u32[]{:S(2)}) collective-permute-start(bf16[2048,64]{1,0:T(8,128)(2,1)S(1)} %collective-permute-done.6), channel_id=1, source_target_pairs={{0,2},{2,4},{4,6},{6,8},{8,10},{10,12},{12,14},{14,16},{16,18},{18... | collective-permute-start | bytes 786440 | tf_op jit(solution)/shard_map/ppermute | solution.py:12
  296.7 0.8 copy-start.4
  297.5 13.7 %collective-permute-start.8 = (bf16[2048,64]{1,0:T(8,128)(2,1)S(1)}, bf16[2048,64]{1,0:T(8,128)(2,1)S(1)}, u32[]{:S(2)}, u32[]{:S(2)}) collective-permute-start(bf16[2048,64]{1,0:T(8,128)(2,1)S(1)} %collective-permute-done.7), channel_id=1, source_target_pairs={{0,2},{2,4},{4,6},{6,8},{8,10},{10,12},{12,14},{14,16},{16,18},{18... | collective-permute-start | bytes 786440 | tf_op jit(solution)/shard_map/ppermute | solution.py:12
  311.2 0.8 copy-start.5
  312.0 15.2 %collective-permute-start.9 = (bf16[2048,64]{1,0:T(8,128)(2,1)S(1)}, bf16[2048,64]{1,0:T(8,128)(2,1)S(1)}, u32[]{:S(2)}, u32[]{:S(2)}) collective-permute-start(bf16[2048,64]{1,0:T(8,128)(2,1)S(1)} %collective-permute-done.8), channel_id=1, source_target_pairs={{0,2},{2,4},{4,6},{6,8},{8,10},{10,12},{12,14},{14,16},{16,18},{18... | collective-permute-start | bytes 786440 | tf_op jit(solution)/shard_map/ppermute | solution.py:12
  327.2 0.8 copy-start.6
  328.0 16.2 %collective-permute-start.10 = (bf16[2048,64]{1,0:T(8,128)(2,1)S(1)}, bf16[2048,64]{1,0:T(8,128)(2,1)S(1)}, u32[]{:S(2)}, u32[]{:S(2)}) collective-permute-start(bf16[2048,64]{1,0:T(8,128)(2,1)S(1)} %collective-permute-done.9), channel_id=1, source_target_pairs={{0,2},{2,4},{4,6},{6,8},{8,10},{10,12},{12,14},{14,16},{16,18},{18... | collective-permute-start | bytes 786440 | tf_op jit(solution)/shard_map/ppermute | solution.py:12
  344.2 0.8 copy-start.7
  345.0 15.8 %collective-permute-start.11 = (bf16[2048,64]{1,0:T(8,128)(2,1)S(1)}, bf16[2048,64]{1,0:T(8,128)(2,1)S(1)}, u32[]{:S(2)}, u32[]{:S(2)}) collective-permute-start(bf16[2048,64]{1,0:T(8,128)(2,1)S(1)} %collective-permute-done.10), channel_id=1, source_target_pairs={{0,2},{2,4},{4,6},{6,8},{8,10},{10,12},{12,14},{14,16},{16,18},{18... | collective-permute-start | bytes 786440 | tf_op jit(solution)/shard_map/ppermute | solution.py:12
  360.8 0.8 copy-start.8
  361.6 14.9 %collective-permute-start.12 = (bf16[2048,64]{1,0:T(8,128)(2,1)S(1)}, bf16[2048,64]{1,0:T(8,128)(2,1)S(1)}, u32[]{:S(2)}, u32[]{:S(2)}) collective-permute-start(bf16[2048,64]{1,0:T(8,128)(2,1)S(1)} %collective-permute-done.11), channel_id=1, source_target_pairs={{0,2},{2,4},{4,6},{6,8},{8,10},{10,12},{12,14},{14,16},{16,18},{18... | collective-permute-start | bytes 786440 | tf_op jit(solution)/shard_map/ppermute | solution.py:12
  376.6 0.8 copy-start.9
  377.4 13.6 %collective-permute-start.13 = (bf16[2048,64]{1,0:T(8,128)(2,1)S(1)}, bf16[2048,64]{1,0:T(8,128)(2,1)}, u32[]{:S(2)}, u32[]{:S(2)}) collective-permute-start(bf16[2048,64]{1,0:T(8,128)(2,1)S(1)} %collective-permute-done.12), channel_id=1, source_target_pairs={{0,2},{2,4},{4,6},{6,8},{8,10},{10,12},{12,14},{14,16},{16,18},{18... | collective-permute-start | bytes 786440 | tf_op jit(solution)/shard_map/ppermute | solution.py:12
  391.0 11.3 %collective-permute-start.14 = (bf16[2048,64]{1,0:T(8,128)(2,1)}, bf16[2048,64]{1,0:T(8,128)(2,1)}, u32[]{:S(2)}, u32[]{:S(2)}) collective-permute-start(bf16[2048,64]{1,0:T(8,128)(2,1)} %collective-permute-done.13), channel_id=1, source_target_pairs={{0,2},{2,4},{4,6},{6,8},{8,10},{10,12},{12,14},{14,16},{16,18},{18... | collective-permute-start | bytes 786440 | tf_op jit(solution)/shard_map/ppermute | solution.py:12
Sparse Core Ops, SparseCore 0:
  32.5 264.5 reduce-scatter.1
